TPU v7x, 32 devices: a whole 2x2x4 slice. The times are simulated.
32 devices in a mesh: slab: 8 (over z, y), batch: 4 (over x, core).
Axes of the slice: x: 2, y: 2, z: 4, core: 2. Of those that a mesh axis runs over, the one named last changes fastest.
Arguments:
- velocity_old: float32 [3, 16, 64, 128], P(None, 'slab', 'batch'), may hold values from -40 to 40
- courant: float32 [3, 16, 64, 128], P(None, 'slab', 'batch'), may hold values from -1.5 to 1.5
- cell_ids: int32 [32768], P(('slab', 'batch')), may hold values from 0 to 16383
- forces: float32 [3, 32768], P(None, ('slab', 'batch')), may hold values from -6 to 6
- weights: float32 [32768], P(('slab', 'batch')), may hold values from 0.25 to 4
Outputs:
- velocity_new: float32 [3, 16, 64, 128], P(None, 'slab', 'batch')
- residual: float32 [3, 16, 64, 128], P(None, 'slab', 'batch')
Inputs may be any that keep to these rules, and one draw needn't show every extreme that they name: `cell_ids`: each device's block of 1024 particles lists 1 * 128 particles for each destination slab in turn, slab 0 first.
All inputs are finite; a program needn't handle non-finite values.
Results may differ from a plain program's by a relative error of at most 0.0012.
Values may be sent and summed in bfloat16 or wider, within the bound.
A program may use at most 64 MiB of HBM per device.

v0:
```python
import math

import jax
import jax.numpy as jnp
from jax import lax
from jax.sharding import PartitionSpec as P

ITERS = 2


diffusion_number = 1.0
diagonal_value = 7.0
deposit_block = 1024


def extended(block, sides, width):
    for axis, dim in sides:
        count = lax.axis_size(axis)
        forward = [(i, i + 1) for i in range(count - 1)]
        backward = [(target, source) for source, target in forward]
        low = lax.ppermute(
            lax.slice_in_dim(block, block.shape[dim] - width, None, axis=dim), axis, forward
        )
        high = lax.ppermute(lax.slice_in_dim(block, 0, width, axis=dim), axis, backward)
        block = jnp.concatenate([low, block, high], axis=dim)
    return block


def inner_product(left, right):
    return jnp.sum(left * right, axis=(1, 2, 3))


def expand(scalars):
    return scalars[:, None, None, None]


def factorize(upper_planes, lower_planes):
    inverses = []
    ratios = []
    for plane_index in range(len(upper_planes)):
        if plane_index == 0:
            pivot_value = diagonal_value + jnp.zeros_like(upper_planes[0])
        else:
            pivot_value = diagonal_value + lower_planes[plane_index] * ratios[-1]
        inverses.append(1.0 / pivot_value)
        ratios.append(-upper_planes[plane_index] * inverses[-1])
    return (inverses, ratios)


def solve_planes(value_planes, inverses, ratios, lower_planes):
    forward = []
    for plane_index in range(len(value_planes)):
        current = value_planes[plane_index]
        if plane_index > 0:
            current = current + lower_planes[plane_index] * forward[-1]
        forward.append(current * inverses[plane_index])
    result = [forward[-1]]
    plane_index = 0
    result.insert(0, forward[plane_index] - ratios[plane_index] * result[0])
    return result


def deposit_rows(cell_ids, momentum, row_total, planes, height, row_width):
    particle_count = cell_ids.shape[0]
    block_size = math.gcd(particle_count, deposit_block)
    row_range = lax.iota(jnp.int32, row_total)
    column_range = lax.iota(jnp.int32, row_width)

    def one_block(iteration, running):
        offset = iteration * block_size
        cell_part = lax.dynamic_slice_in_dim(cell_ids, offset, block_size, 0)
        momentum_part = lax.dynamic_slice_in_dim(momentum, offset, block_size, 1)
        plane_index = cell_part // (height * row_width)
        row_number = cell_part // row_width % height
        column = cell_part % row_width
        local_row = row_number * planes + plane_index
        row_hot = (local_row[:, None] == row_range[None, :]).astype(jnp.bfloat16)
        column_hot = column[:, None] == column_range[None, :]
        spread = jnp.where(
            column_hot[:, None, :], momentum_part.T[:, :, None], jnp.zeros((), jnp.bfloat16)
        )
        spread = spread.reshape(block_size, 3 * row_width)
        return running + jnp.einsum(
            "pr,pc->rc", row_hot, spread, preferred_element_type=jnp.float32
        )

    initial = jnp.zeros((row_total, 3 * row_width), jnp.float32)
    return lax.fori_loop(0, particle_count // block_size, one_block, initial)


def local(velocity_old, courant, cell_ids, forces, weights):
    planes = velocity_old.shape[1]
    rows_quarter = velocity_old.shape[2]
    row_width = velocity_old.shape[3]
    height = rows_quarter * lax.axis_size("batch")
    block_rows = planes * rows_quarter
    momentum = (weights[None, :] * forces).astype(jnp.bfloat16)
    ids_here = lax.all_to_all(cell_ids, "slab", split_axis=0, concat_axis=0, tiled=True)
    moved_momentum = lax.all_to_all(momentum, "slab", split_axis=1, concat_axis=1, tiled=True)
    summed = lax.psum_scatter(
        deposit_rows(
            ids_here, moved_momentum, block_rows * lax.axis_size("batch"), planes, height, row_width
        ),
        "batch",
        scatter_dimension=0,
        tiled=True,
    )
    source = summed.reshape(rows_quarter, planes, 3, row_width).transpose(2, 1, 0, 3)
    right_side = velocity_old + source
    upper = diffusion_number - 0.5 * courant
    lower = diffusion_number + 0.5 * courant
    upper_planes = [upper[0, plane_index] for plane_index in range(planes)]
    lower_planes = [lower[0, plane_index] for plane_index in range(planes)]
    inverses, ratios = factorize(upper_planes, lower_planes)

    def operate(values):
        padded = extended(values, (("slab", 1), ("batch", 2)), 1)
        edge_zeros = jnp.zeros_like(values[..., :1])
        plus_x = jnp.concatenate([values[..., 1:], edge_zeros], axis=3)
        minus_x = jnp.concatenate([edge_zeros, values[..., :-1]], axis=3)
        beside = upper[0] * padded[:, 2:, 1:-1] + lower[0] * padded[:, :-2, 1:-1]
        beside = beside + upper[1] * padded[:, 1:-1, 2:] + lower[1] * padded[:, 1:-1, :-2]
        beside = beside + upper[2] * plus_x + lower[2] * minus_x
        return diagonal_value * values - beside

    def precondition(values):
        value_planes = [values[:, plane_index] for plane_index in range(planes)]
        result = solve_planes(value_planes, inverses, ratios, lower_planes)
        return jnp.stack(result, axis=1)

    solution = jnp.zeros_like(right_side)
    residual = right_side
    direction = right_side
    rho_now = None
    for iteration in range(ITERS):
        precond_dir = precondition(direction)
        image_dir = operate(precond_dir)
        if iteration == 0:
            stacked_terms = jnp.stack(
                [inner_product(right_side, image_dir), inner_product(right_side, residual)], axis=0
            )
        else:
            stacked_terms = inner_product(right_side, image_dir)[None, :]
        gathered_sums = lax.psum(stacked_terms, ("slab", "batch"))
        along_sum = gathered_sums[0]
        if iteration == 0:
            rho_now = gathered_sums[1]
        step_alpha = rho_now / along_sum
        middle = residual - expand(step_alpha) * image_dir
        precond_mid = precondition(middle)
        turned = operate(precond_mid)
        term_list = [inner_product(turned, middle), inner_product(turned, turned)]
        if iteration + 1 < ITERS:
            term_list.append(inner_product(right_side, turned))
        closing_sums = lax.psum(jnp.stack(term_list, axis=0), ("slab", "batch"))
        cross_sum = closing_sums[0]
        square = closing_sums[1]
        shadow_turned = closing_sums[2] if iteration + 1 < ITERS else None
        step_omega = cross_sum / square
        solution = solution + expand(step_alpha) * precond_dir + expand(step_omega) * precond_mid
        residual = middle - expand(step_omega) * turned
        if iteration + 1 < ITERS:
            rho_next = rho_now - step_alpha * along_sum - step_omega * shadow_turned
            factor = rho_next / rho_now * (step_alpha / step_omega)
            direction = residual + expand(factor) * (direction - expand(step_omega) * image_dir)
            rho_now = rho_next
    return (solution, residual)


def solution(mesh):
    placed = (
        P(None, "slab", "batch", None),
        P(None, "slab", "batch", None),
        P(("slab", "batch")),
        P(None, ("slab", "batch")),
        P(("slab", "batch")),
    )
    return jax.shard_map(
        local,
        mesh=mesh,
        in_specs=placed,
        out_specs=(P(None, "slab", "batch", None), P(None, "slab", "batch", None)),
        check_vma=False,
    )
```

profile of v0, /device:TPU:0, one launch (start us, length us, event | category | flops | bytes accessed | tf_op | source)
XLA Modules:
  0.0 286.1 jit_solution(11093976552176510271)
XLA Ops:
  7.2 7.3 %all-to-all-start = ((s32[8,128,1]{1,2,0:T(1,128)}), s32[8,128,1]{1,2,0:T(1,128)S(1)}, u32[]{:S(2)}, u32[]{:S(2)}) async-start(s32[8,128,1]{1,2,0:T(1,128)} %bitcast.93), calls=%async_computation | async-start | bytes 8192 | tf_op jit(solution)/shard_map/all_to_all | solution.py:98
  14.5 0.8 multiply_add_fusion.2
  15.3 0.6 fusion.48
  16.0 5.0 %all-to-all-done = s32[8,128,1]{1,2,0:T(1,128)S(1)} async-done(((s32[8,128,1]{1,2,0:T(1,128)}), s32[8,128,1]{1,2,0:T(1,128)S(1)}, u32[]{:S(2)}, u32[]{:S(2)}) %all-to-all-start) | async-done | bytes 4128 | tf_op jit(solution)/shard_map/all_to_all | solution.py:98
  20.9 3.3 %all-to-all-start.1 = ((bf16[3,8,128]{2,0,1:T(4,128)(2,1)}), bf16[3,8,128]{2,0,1:T(4,128)(2,1)S(1)}, u32[]{:S(2)}, u32[]{:S(2)}) async-start(bf16[3,8,128]{2,0,1:T(4,128)(2,1)} %fusion.48), calls=%async_computation.1 | async-start | bytes 16384 | tf_op jit(solution)/shard_map/all_to_all | solution.py:99
  24.4 6.3 %all-to-all-done.1 = bf16[3,8,128]{2,0,1:T(4,128)(2,1)S(1)} async-done(((bf16[3,8,128]{2,0,1:T(4,128)(2,1)}), bf16[3,8,128]{2,0,1:T(4,128)(2,1)S(1)}, u32[]{:S(2)}, u32[]{:S(2)}) %all-to-all-start.1) | async-done | bytes 6176 | tf_op jit(solution)/shard_map/all_to_all | solution.py:99
  30.8 1.3 fusion.1
  32.1 17.2 %reduce-scatter.2.cloned.1.call-done = f32[32,384]{1,0:T(8,128)} async-done(((f32[128,384]{1,0:T(8,128)}), f32[32,384]{1,0:T(8,128)}) %reduce-scatter.2.cloned.1.call-update) | async-done | bytes 49168 | tf_op jit(solution)/shard_map/reduce_scatter | solution.py:100
  49.3 0.8 reshape.219
  50.2 1.3 collective-permute-start
  51.5 4.5 %collective-permute-start.1 = (f32[3,1,16,128]{3,0,1,2:T(4,128)S(1)}, f32[3,1,16,128]{3,0,1,2:T(4,128)S(1)}, u32[]{:S(2)}, u32[]{:S(2)}) collective-permute-start(f32[3,1,16,128]{3,0,1,2:T(4,128)S(1)} %get-tuple-element.75), channel_id=1, source_target_pairs={{0,4},{4,8},{8,12},{12,16},{16,20},{20,24},{24,28},{1,5},{5,9},{9,... | collective-permute-start | bytes 73736 | tf_op jit(solution)/shard_map/ppermute | solution.py:21
  56.2 1.4 collective-permute-done.1
  57.6 1.3 collective-permute-start.3
  58.9 1.3 collective-permute-start.2
  60.2 0.1 fusion.10
  60.3 2.2 collective-permute-done.2
  62.5 0.2 multiply_reduce_fusion.7
  62.7 42.7 %psum.28 = f32[2,3]{1,0:T(2,128)S(1)} all-reduce(f32[2,3]{1,0:T(2,128)S(1)} %pad_maximum_fusion.53), channel_id=1, replica_groups=mesh['slab'=8,'batch'=4] {'slab','batch'}, use_global_device_ids=true, to_apply=%region_3.4 | all-reduce | flops 6 | bytes 48 | tf_op jit(solution)/shard_map/psum | solution.py:144
  105.5 1.3 collective-permute-start.4
  106.8 4.8 %collective-permute-start.5 = (f32[3,1,16,128]{3,0,1,2:T(4,128)S(1)}, f32[3,1,16,128]{3,0,1,2:T(4,128)S(1)}, u32[]{:S(2)}, u32[]{:S(2)}) collective-permute-start(f32[3,1,16,128]{3,0,1,2:T(4,128)S(1)} %get-tuple-element.72), channel_id=1, source_target_pairs={{0,4},{4,8},{8,12},{12,16},{16,20},{20,24},{24,28},{1,5},{5,9},{9,... | collective-permute-start | bytes 73736 | tf_op jit(solution)/shard_map/ppermute | solution.py:21
  111.7 1.6 collective-permute-done.5
  113.2 1.3 collective-permute-start.7
  114.5 1.3 collective-permute-start.6
  115.8 0.1 fusion.8
  115.9 3.9 %collective-permute-done.6 = f32[3,4,1,128]{3,0,1,2:T(4,128)S(1)} collective-permute-done((f32[3,4,1,128]{3,0,1,2:T(4,128)S(1)}, f32[3,4,1,128]{3,0,1,2:T(4,128)S(1)}, u32[]{:S(2)}, u32[]{:S(2)}) %collective-permute-start.6) | collective-permute-done | bytes 6176 | tf_op jit(solution)/shard_map/ppermute | solution.py:24
  119.9 0.3 multiply_reduce_fusion.5
  120.2 42.8 %psum.29 = f32[3,3]{1,0:T(4,128)S(1)} all-reduce(f32[3,3]{1,0:T(4,128)S(1)} %pad_maximum_fusion.52), channel_id=1, replica_groups=mesh['slab'=8,'batch'=4] {'slab','batch'}, use_global_device_ids=true, to_apply=%region_7.8 | all-reduce | flops 9 | bytes 72 | tf_op jit(solution)/shard_map/psum | solution.py:155
  163.0 0.1 multiply_add_fusion.1
  163.1 1.3 collective-permute-start.8
  164.4 4.8 %collective-permute-start.9 = (f32[3,1,16,128]{3,0,1,2:T(4,128)S(1)}, f32[3,1,16,128]{3,0,1,2:T(4,128)S(1)}, u32[]{:S(2)}, u32[]{:S(2)}) collective-permute-start(f32[3,1,16,128]{3,0,1,2:T(4,128)S(1)} %get-tuple-element.66), channel_id=1, source_target_pairs={{0,4},{4,8},{8,12},{12,16},{16,20},{20,24},{24,28},{1,5},{5,9},{9,... | collective-permute-start | bytes 73736 | tf_op jit(solution)/shard_map/ppermute | solution.py:21
  169.3 1.6 collective-permute-done.9
  170.8 1.3 collective-permute-start.11
  172.1 1.3 collective-permute-start.10
  173.4 0.1 fusion.6
  173.5 3.9 %collective-permute-done.10 = f32[3,4,1,128]{3,0,1,2:T(4,128)S(1)} collective-permute-done((f32[3,4,1,128]{3,0,1,2:T(4,128)S(1)}, f32[3,4,1,128]{3,0,1,2:T(4,128)S(1)}, u32[]{:S(2)}, u32[]{:S(2)}) %collective-permute-start.10) | collective-permute-done | bytes 6176 | tf_op jit(solution)/shard_map/ppermute | solution.py:24
  177.4 0.2 multiply_reduce_fusion.2
  177.7 42.8 %psum.30 = f32[3]{0:T(128)S(1)} all-reduce(f32[3]{0:T(128)S(1)} %get-tuple-element.63), channel_id=1, replica_groups=mesh['slab'=8,'batch'=4] {'slab','batch'}, use_global_device_ids=true, to_apply=%region_9.10 | all-reduce | flops 3 | bytes 24 | tf_op jit(solution)/shard_map/psum | solution.py:144
  220.6 1.3 collective-permute-start.12
  221.9 4.8 %collective-permute-start.13 = (f32[3,1,16,128]{3,0,1,2:T(4,128)S(1)}, f32[3,1,16,128]{3,0,1,2:T(4,128)S(1)}, u32[]{:S(2)}, u32[]{:S(2)}) collective-permute-start(f32[3,1,16,128]{3,0,1,2:T(4,128)S(1)} %get-tuple-element.62), channel_id=1, source_target_pairs={{0,4},{4,8},{8,12},{12,16},{16,20},{20,24},{24,28},{1,5},{5,9},{9,... | collective-permute-start | bytes 73736 | tf_op jit(solution)/shard_map/ppermute | solution.py:21
  226.7 1.6 collective-permute-done.13
  228.3 1.3 collective-permute-start.15
  229.6 1.3 collective-permute-start.14
  231.0 3.9 %collective-permute-done.14 = f32[3,4,1,128]{3,0,1,2:T(4,128)S(1)} collective-permute-done((f32[3,4,1,128]{3,0,1,2:T(4,128)S(1)}, f32[3,4,1,128]{3,0,1,2:T(4,128)S(1)}, u32[]{:S(2)}, u32[]{:S(2)}) %collective-permute-start.14) | collective-permute-done | bytes 6176 | tf_op jit(solution)/shard_map/ppermute | solution.py:24
  234.9 0.2 multiply_reduce_fusion.1
  235.1 42.7 %psum.31 = f32[2,3]{1,0:T(2,128)S(1)} all-reduce(f32[2,3]{1,0:T(2,128)S(1)} %pad_maximum_fusion.54), channel_id=1, replica_groups=mesh['slab'=8,'batch'=4] {'slab','batch'}, use_global_device_ids=true, to_apply=%region_12.13 | all-reduce | flops 6 | bytes 48 | tf_op jit(solution)/shard_map/psum | solution.py:155
  277.9 0.1 multiply_subtract_fusion
  278.0 0.6 copy.26
  278.7 0.6 copy.27
  (47 shorter events, 0.9 us)
Async XLA Ops:
  7.2 13.7 %all-to-all-start = ((s32[8,128,1]{1,2,0:T(1,128)}), s32[8,128,1]{1,2,0:T(1,128)S(1)}, u32[]{:S(2)}, u32[]{:S(2)}) async-start(s32[8,128,1]{1,2,0:T(1,128)} %bitcast.93), calls=%async_computation | async-start | bytes 8192 | tf_op jit(solution)/shard_map/all_to_all | solution.py:98
  14.5 0.8 copy-start.1
  14.5 0.8 copy-start.2
  20.9 9.8 %all-to-all-start.1 = ((bf16[3,8,128]{2,0,1:T(4,128)(2,1)}), bf16[3,8,128]{2,0,1:T(4,128)(2,1)S(1)}, u32[]{:S(2)}, u32[]{:S(2)}) async-start(bf16[3,8,128]{2,0,1:T(4,128)(2,1)} %fusion.48), calls=%async_computation.1 | async-start | bytes 16384 | tf_op jit(solution)/shard_map/all_to_all | solution.py:99
  24.2 25.0 %reduce-scatter.2.cloned.1.call-start = ((), (), s32[]{:S(2)}) async-start(), calls=%async_computation.3 | async-start | bytes 245760 | tf_op jit(solution)/shard_map/reduce_scatter | solution.py:100
  32.1 18.0 %copy-start = (f32[3,2,16,128]{3,2,1,0:T(8,128)S(1)}, f32[3,2,16,128]{3,2,1,0:T(8,128)}, u32[]{:S(2)}) copy-start(f32[3,2,16,128]{3,2,1,0:T(8,128)} %param.5) | copy-start | bytes 147460
  50.2 6.0 %collective-permute-start = (f32[3,1,16,128]{3,0,1,2:T(4,128)S(1)}, f32[3,1,16,128]{3,0,1,2:T(4,128)S(1)}, u32[]{:S(2)}, u32[]{:S(2)}) collective-permute-start(f32[3,1,16,128]{3,0,1,2:T(4,128)S(1)} %get-tuple-element.74), channel_id=1, source_target_pairs={{4,0},{8,4},{12,8},{16,12},{20,16},{24,20},{28,24},{5,1},{9,5},{13... | collective-permute-start | bytes 73736 | tf_op jit(solution)/shard_map/ppermute | solution.py:24
  51.5 6.1 %collective-permute-start.1 = (f32[3,1,16,128]{3,0,1,2:T(4,128)S(1)}, f32[3,1,16,128]{3,0,1,2:T(4,128)S(1)}, u32[]{:S(2)}, u32[]{:S(2)}) collective-permute-start(f32[3,1,16,128]{3,0,1,2:T(4,128)S(1)} %get-tuple-element.75), channel_id=1, source_target_pairs={{0,4},{4,8},{8,12},{12,16},{16,20},{20,24},{24,28},{1,5},{5,9},{9,... | collective-permute-start | bytes 73736 | tf_op jit(solution)/shard_map/ppermute | solution.py:21
  57.6 2.7 collective-permute-start.3
  58.9 3.6 %collective-permute-start.2 = (f32[3,4,1,128]{3,0,1,2:T(4,128)S(1)}, f32[3,4,1,128]{3,0,1,2:T(4,128)S(1)}, u32[]{:S(2)}, u32[]{:S(2)}) collective-permute-start(f32[3,4,1,128]{3,0,1,2:T(4,128)S(1)} %get-tuple-element.82), channel_id=1, source_target_pairs={{1,0},{2,1},{3,2},{5,4},{6,5},{7,6},{9,8},{10,9},{11,10},{13,12},{... | collective-permute-start | bytes 18440 | tf_op jit(solution)/shard_map/ppermute | solution.py:24
  105.5 6.1 %collective-permute-start.4 = (f32[3,1,16,128]{3,0,1,2:T(4,128)S(1)}, f32[3,1,16,128]{3,0,1,2:T(4,128)S(1)}, u32[]{:S(2)}, u32[]{:S(2)}) collective-permute-start(f32[3,1,16,128]{3,0,1,2:T(4,128)S(1)} %get-tuple-element.71), channel_id=1, source_target_pairs={{4,0},{8,4},{12,8},{16,12},{20,16},{24,20},{28,24},{5,1},{9,5},{13... | collective-permute-start | bytes 73736 | tf_op jit(solution)/shard_map/ppermute | solution.py:24
  106.8 6.4 %collective-permute-start.5 = (f32[3,1,16,128]{3,0,1,2:T(4,128)S(1)}, f32[3,1,16,128]{3,0,1,2:T(4,128)S(1)}, u32[]{:S(2)}, u32[]{:S(2)}) collective-permute-start(f32[3,1,16,128]{3,0,1,2:T(4,128)S(1)} %get-tuple-element.72), channel_id=1, source_target_pairs={{0,4},{4,8},{8,12},{12,16},{16,20},{20,24},{24,28},{1,5},{5,9},{9,... | collective-permute-start | bytes 73736 | tf_op jit(solution)/shard_map/ppermute | solution.py:21
  113.2 2.7 collective-permute-start.7
  114.5 5.3 %collective-permute-start.6 = (f32[3,4,1,128]{3,0,1,2:T(4,128)S(1)}, f32[3,4,1,128]{3,0,1,2:T(4,128)S(1)}, u32[]{:S(2)}, u32[]{:S(2)}) collective-permute-start(f32[3,4,1,128]{3,0,1,2:T(4,128)S(1)} %get-tuple-element.80), channel_id=1, source_target_pairs={{1,0},{2,1},{3,2},{5,4},{6,5},{7,6},{9,8},{10,9},{11,10},{13,12},{... | collective-permute-start | bytes 18440 | tf_op jit(solution)/shard_map/ppermute | solution.py:24
  163.1 6.1 %collective-permute-start.8 = (f32[3,1,16,128]{3,0,1,2:T(4,128)S(1)}, f32[3,1,16,128]{3,0,1,2:T(4,128)S(1)}, u32[]{:S(2)}, u32[]{:S(2)}) collective-permute-start(f32[3,1,16,128]{3,0,1,2:T(4,128)S(1)} %get-tuple-element.65), channel_id=1, source_target_pairs={{4,0},{8,4},{12,8},{16,12},{20,16},{24,20},{28,24},{5,1},{9,5},{13... | collective-permute-start | bytes 73736 | tf_op jit(solution)/shard_map/ppermute | solution.py:24
  164.4 6.4 %collective-permute-start.9 = (f32[3,1,16,128]{3,0,1,2:T(4,128)S(1)}, f32[3,1,16,128]{3,0,1,2:T(4,128)S(1)}, u32[]{:S(2)}, u32[]{:S(2)}) collective-permute-start(f32[3,1,16,128]{3,0,1,2:T(4,128)S(1)} %get-tuple-element.66), channel_id=1, source_target_pairs={{0,4},{4,8},{8,12},{12,16},{16,20},{20,24},{24,28},{1,5},{5,9},{9,... | collective-permute-start | bytes 73736 | tf_op jit(solution)/shard_map/ppermute | solution.py:21
  170.8 2.7 collective-permute-start.11
  172.1 5.3 %collective-permute-start.10 = (f32[3,4,1,128]{3,0,1,2:T(4,128)S(1)}, f32[3,4,1,128]{3,0,1,2:T(4,128)S(1)}, u32[]{:S(2)}, u32[]{:S(2)}) collective-permute-start(f32[3,4,1,128]{3,0,1,2:T(4,128)S(1)} %get-tuple-element.78), channel_id=1, source_target_pairs={{1,0},{2,1},{3,2},{5,4},{6,5},{7,6},{9,8},{10,9},{11,10},{13,12},{... | collective-permute-start | bytes 18440 | tf_op jit(solution)/shard_map/ppermute | solution.py:24
  220.6 6.1 %collective-permute-start.12 = (f32[3,1,16,128]{3,0,1,2:T(4,128)S(1)}, f32[3,1,16,128]{3,0,1,2:T(4,128)S(1)}, u32[]{:S(2)}, u32[]{:S(2)}) collective-permute-start(f32[3,1,16,128]{3,0,1,2:T(4,128)S(1)} %get-tuple-element.61), channel_id=1, source_target_pairs={{4,0},{8,4},{12,8},{16,12},{20,16},{24,20},{28,24},{5,1},{9,5},{13... | collective-permute-start | bytes 73736 | tf_op jit(solution)/shard_map/ppermute | solution.py:24
  221.9 6.4 %collective-permute-start.13 = (f32[3,1,16,128]{3,0,1,2:T(4,128)S(1)}, f32[3,1,16,128]{3,0,1,2:T(4,128)S(1)}, u32[]{:S(2)}, u32[]{:S(2)}) collective-permute-start(f32[3,1,16,128]{3,0,1,2:T(4,128)S(1)} %get-tuple-element.62), channel_id=1, source_target_pairs={{0,4},{4,8},{8,12},{12,16},{16,20},{20,24},{24,28},{1,5},{5,9},{9,... | collective-permute-start | bytes 73736 | tf_op jit(solution)/shard_map/ppermute | solution.py:21
  228.3 2.7 collective-permute-start.15
  229.6 5.3 %collective-permute-start.14 = (f32[3,4,1,128]{3,0,1,2:T(4,128)S(1)}, f32[3,4,1,128]{3,0,1,2:T(4,128)S(1)}, u32[]{:S(2)}, u32[]{:S(2)}) collective-permute-start(f32[3,4,1,128]{3,0,1,2:T(4,128)S(1)} %get-tuple-element.76), channel_id=1, source_target_pairs={{1,0},{2,1},{3,2},{5,4},{6,5},{7,6},{9,8},{10,9},{11,10},{13,12},{... | collective-permute-start | bytes 18440 | tf_op jit(solution)/shard_map/ppermute | solution.py:24
Sparse Core Ops, SparseCore 0:
  32.2 17.0 reduce-scatter.1
where the time goes:
time: 287 us; the launch traced here: 286 us
  blocking collectives  171 us (60%)
  waiting for transfers between devices  48.5 us (17%)
  starting transfers between devices  45.1 us (16%)
  between operations  14.5 us (5%)
  other arithmetic  3.66 us (1%)
    psum x2, blocking collectives, local(): closing_sums = lax.psum(jnp.stack(term_list, axis=0), ('slab', 'batch'))  85.6 us
    psum x2, blocking collectives, local(): gathered_sums = lax.psum(stacked_terms, ('slab', 'batch'))  85.4 us
    ppermute x8, starting transfers between devices, extended(): lax.ppermute(lax.slice_in_dim(block, block.shape[dim] - width, None, axis...  24.1 us
    reduce_scatter x1, waiting for transfers between devices, local(): lax.psum_scatter(deposit_rows(ids_here, moved_momentum, block_rows * lax....  17.2 us
    ppermute x8, waiting for transfers between devices, extended(): lax.ppermute(lax.slice_in_dim(block, 0, width, axis=dim), axis, backward)  13.9 us
    ppermute x8, starting transfers between devices, extended(): lax.ppermute(lax.slice_in_dim(block, 0, width, axis=dim), axis, backward)  10.3 us
    all_to_all x1, starting transfers between devices, local(): lax.all_to_all(cell_ids, 'slab', split_axis=0, concat_axis=0, tiled=True)  7.32 us
    all_to_all x1, waiting for transfers between devices, local(): lax.all_to_all(momentum, 'slab', split_axis=1, concat_axis=1, tiled=True)  6.3 us
  transfers between devices with their start and end apart: 19, of which 11 were waited for; matrix products, arithmetic and copies ran while one was open for 1% of the time, Pallas kernels for 0%

commit v1 on v0

v1 whole, which is shorter than its diff:
```python
import functools

import jax
import jax.numpy as jnp
from jax import lax
from jax.experimental import pallas as pl
from jax.experimental.pallas import tpu as pltpu
from jax.sharding import PartitionSpec as P

MESH = pl.DeviceIdType.MESH
diffusion_number = 1.0
diagonal_value = 7.0
COMPS = 3
STEPS = 4
FIELDS = COMPS + 1
group_size = 8


def kernel(
    slabs, groups,
    velocity, courant, cells, forces, weights,
    out_velocity, out_residual,
    pack, arrived, plane_out, plane_low, plane_high, row_out, row_low, row_high,
    sums_out, sums_in,
    part_sems, halo_send, halo_recv, sum_sems,
):
    planes, rows, width = velocity.shape[1:]
    count = slabs * groups
    per_slab = cells.shape[1]
    slab, group = lax.axis_index("slab"), lax.axis_index("batch")
    me = slab * groups + group

    def place(index):
        return {"slab": index // groups, "batch": lax.rem(index, groups)}

    def others(visit):
        def step(offset, carry):
            visit(lax.rem(me + offset, count))
            return carry
        lax.fori_loop(1, count, step, 0)

    barrier = pltpu.get_barrier_semaphore()
    others(lambda peer: pl.semaphore_signal(
        barrier, inc=1, device_id=place(peer), device_id_type=MESH))

    for target in range(slabs):
        span = slice(target * per_slab, (target + 1) * per_slab)
        moved = (weights[target:target + 1, :] * forces[:, span]).astype(jnp.bfloat16)
        pack[target, 0:COMPS, :] = moved.astype(jnp.float32)
        pack[target, COMPS:FIELDS, :] = cells[target:target + 1, :].astype(jnp.float32)
    arrived[me] = pack[slab]

    def zero(ref):
        ref[...] = jnp.zeros(ref.shape, ref.dtype)

    pl.when(slab == 0)(lambda: zero(plane_low))
    pl.when(slab == slabs - 1)(lambda: zero(plane_high))
    pl.when(group == 0)(lambda: zero(row_low))
    pl.when(group == groups - 1)(lambda: zero(row_high))

    pl.semaphore_wait(barrier, count - 1)

    def send_particles(peer):
        pltpu.make_async_remote_copy(
            src_ref=pack.at[peer // groups], dst_ref=arrived.at[me],
            send_sem=part_sems.at[0], recv_sem=part_sems.at[1],
            device_id=place(peer), device_id_type=MESH,
        ).start()

    others(send_particles)

    lane = lax.broadcasted_iota(jnp.int32, (rows, width), 1)
    line = lax.broadcasted_iota(jnp.int32, (rows, width), 0)
    upper = [[diffusion_number - 0.5 * courant[d, z] for z in range(planes)] for d in range(3)]
    lower = [[diffusion_number + 0.5 * courant[d, z] for z in range(planes)] for d in range(3)]
    none = jnp.zeros((rows, width), jnp.float32)
    x_next = [jnp.where(lane == width - 1, none, c) for c in upper[2]]
    x_prev = [jnp.where(lane == 0, none, c) for c in lower[2]]
    y_next = [jnp.where(line == rows - 1, none, c) for c in upper[1]]
    y_prev = [jnp.where(line == 0, none, c) for c in lower[1]]
    y_next_edge = [jnp.where(line == rows - 1, c, none) for c in upper[1]]
    y_prev_edge = [jnp.where(line == 0, c, none) for c in lower[1]]
    inverses, ratios = [], []
    for z in range(planes):
        pivot = diagonal_value + (none if z == 0 else lower[0][z] * ratios[-1])
        inverses.append(1.0 / pivot)
        ratios.append(-upper[0][z] * inverses[-1])

    def precondition(v):
        result = [[None] * COMPS for _ in range(planes)]
        for k in range(COMPS):
            forward = []
            for z in range(planes):
                current = v[z][k]
                if z > 0:
                    current = current + lower[0][z] * forward[-1]
                forward.append(current * inverses[z])
            result[planes - 1][k] = forward[-1]
            for z in range(planes - 2, -1, -1):
                result[z][k] = forward[z] - ratios[z] * result[z + 1][k]
        return result

    def halo_copies(step):
        def copy(which, src, dst, peer):
            return pltpu.make_async_remote_copy(
                src_ref=src, dst_ref=dst,
                send_sem=halo_send.at[step, which], recv_sem=halo_recv.at[step, which],
                device_id=peer, device_id_type=MESH)
        return (
            (copy(0, plane_out.at[step, 0], plane_high.at[step], {"slab": slab - 1, "batch": group}), slab > 0, slab < slabs - 1),
            (copy(1, plane_out.at[step, 1], plane_low.at[step], {"slab": slab + 1, "batch": group}), slab < slabs - 1, slab > 0),
            (copy(2, row_out.at[step, 0], row_high.at[step], {"slab": slab, "batch": group - 1}), group > 0, group < groups - 1),
            (copy(3, row_out.at[step, 1], row_low.at[step], {"slab": slab, "batch": group + 1}), group < groups - 1, group > 0),
        )

    def start_halo(step, u):
        for k in range(COMPS):
            plane_out[step, 0, k] = u[0][k]
            plane_out[step, 1, k] = u[planes - 1][k]
            for z in range(planes):
                at = z * COMPS + k
                row_out[step, 0, at:at + 1] = u[z][k][0:1]
                row_out[step, 1, at:at + 1] = u[z][k][rows - 1:rows]
        for copy, sends, _ in halo_copies(step):
            pl.when(sends)(copy.start)

    def inner_part(u):
        result = []
        for z in range(planes):
            line_of = []
            for k in range(COMPS):
                c = u[z][k]
                beside = x_next[z] * pltpu.roll(c, width - 1, 1) + x_prev[z] * pltpu.roll(c, 1, 1)
                beside = beside + y_next[z] * pltpu.roll(c, rows - 1, 0) + y_prev[z] * pltpu.roll(c, 1, 0)
                if z + 1 < planes:
                    beside = beside + upper[0][z] * u[z + 1][k]
                if z > 0:
                    beside = beside + lower[0][z] * u[z - 1][k]
                line_of.append(diagonal_value * c - beside)
            result.append(line_of)
        return result

    def finish(step, partial):
        for copy, _, receives in halo_copies(step):
            pl.when(receives)(copy.wait_recv)
        result = []
        for z in range(planes):
            line_of = []
            for k in range(COMPS):
                at = z * COMPS + k
                value = partial[z][k]
                value = value - y_next_edge[z] * row_high[step, at:at + 1]
                value = value - y_prev_edge[z] * row_low[step, at:at + 1]
                if z == planes - 1:
                    value = value - upper[0][z] * plane_high[step, k]
                if z == 0:
                    value = value - lower[0][z] * plane_low[step, k]
                line_of.append(value)
            result.append(line_of)
        return result

    sum_lane = lax.broadcasted_iota(jnp.int32, (8, width), 1)

    def add_products(total, first, pairs):
        for offset, (left, right) in enumerate(pairs):
            for k in range(COMPS):
                terms = sum(left[z][k] * right[z][k] for z in range(planes))
                folded = sum(terms[r:r + 8] for r in range(0, rows, 8))
                lanes = jnp.sum(folded, axis=1, keepdims=True)
                total = jnp.where(sum_lane == COMPS * (first + offset) + k, lanes, total)
        return total

    def start_sums(which, total):
        row = jnp.sum(total, axis=0, keepdims=True)
        sums_out[which] = row
        sums_in[which, me] = row

        def send(peer):
            pltpu.make_async_remote_copy(
                src_ref=sums_out.at[which], dst_ref=sums_in.at[which, me],
                send_sem=sum_sems.at[which, 0], recv_sem=sum_sems.at[which, 1],
                device_id=place(peer), device_id_type=MESH,
            ).start()

        others(send)

    def await_bytes(ref, sem):
        pltpu.make_async_copy(ref, ref, sem).wait()

    def finish_sums(which, entries):
        await_bytes(sums_in.at[which, pl.ds(0, count - 1)], sum_sems.at[which, 1])
        total = jnp.sum(sums_in[which], axis=0)
        total = jnp.broadcast_to(total, (8, width))
        return [total if p == 0 else pltpu.roll(total, width - COMPS * p, 1) for p in range(entries)]

    def scale(coefficient):
        return [coefficient[0:1, k:k + 1] for k in range(COMPS)]

    def combine(base, coefficient, other):
        return [[base[z][k] + coefficient[k] * other[z][k] for k in range(COMPS)] for z in range(planes)]

    await_bytes(arrived.at[pl.ds(0, count - 1)], part_sems.at[1])
    spot = lax.broadcasted_iota(jnp.int32, (planes * rows, per_slab), 0)
    wanted = (spot // rows * (rows * groups) + group * rows + lax.rem(spot, rows)).astype(jnp.float32)
    column_of = lax.broadcasted_iota(jnp.int32, (width, per_slab), 0).astype(jnp.float32)

    def deposit(first, running):
        values, columns = [], []
        for item in range(group_size):
            block = arrived[first * group_size + item]
            cell = block[COMPS:FIELDS]
            row_number = jnp.floor(cell * (1.0 / width))
            column = cell - row_number * width
            hit = row_number == wanted
            values.append(jnp.concatenate(
                [jnp.where(hit, block[k:k + 1], 0.0) for k in range(COMPS)], axis=0).astype(jnp.bfloat16))
            columns.append(jnp.where(column == column_of, 1.0, 0.0).astype(jnp.bfloat16))
        return running + lax.dot_general(
            jnp.concatenate(values, axis=1), jnp.concatenate(columns, axis=1),
            (((1,), (1,)), ((), ())), preferred_element_type=jnp.float32)

    source = jnp.zeros((COMPS * planes * rows, width), jnp.float32)
    if count <= 8 * group_size:
        for first in range(count // group_size):
            source = deposit(first, source)
    else:
        source = lax.fori_loop(0, count // group_size, deposit, source)

    w0 = [[velocity[k, z] + source[(k * planes + z) * rows:(k * planes + z + 1) * rows]
           for k in range(COMPS)] for z in range(planes)]

    u0 = precondition(w0)
    start_halo(0, u0)
    total = add_products(jnp.zeros((8, width), jnp.float32), 0, [(w0, w0)])
    w1 = finish(0, inner_part(u0))
    u1 = precondition(w1)
    start_halo(1, u1)
    total = add_products(total, 1, [(w0, w1), (w1, w1)])
    w2 = finish(1, inner_part(u1))
    u2 = precondition(w2)
    start_halo(2, u2)
    start_sums(0, add_products(total, 3, [(w0, w2), (w1, w2), (w2, w2)]))
    w3 = finish(2, inner_part(u2))
    g00, g01, g11, g02, g12, g22 = finish_sums(0, 6)
    alpha = g00 / g01
    omega = ((g01 - alpha * g02) - alpha * (g11 - alpha * g12)) / (g11 - alpha * (2.0 * g12 - alpha * g22))
    rho = g00 - alpha * g01 - omega * (g01 - alpha * g02)
    factor = rho / g00 * (alpha / omega)
    plus_alpha, plus_omega, plus_factor = scale(alpha), scale(omega), scale(factor)
    less_alpha, less_omega = scale(-alpha), scale(-omega)
    middle_u = combine(u0, less_alpha, u1)
    turned = combine(w1, less_alpha, w2)
    residual = combine(combine(w0, less_alpha, w1), less_omega, turned)
    residual_u = combine(middle_u, less_omega, combine(u1, less_alpha, u2))
    residual_image = combine(turned, less_omega, combine(w2, less_alpha, w3))

    image = combine(residual_image, plus_factor, combine(w1, less_omega, w2))
    image_u = precondition(image)
    start_halo(3, image_u)
    total = add_products(jnp.zeros((8, width), jnp.float32), 0, [
        (w0, image), (residual_image, residual), (residual_image, image), (residual_image, residual_image)])
    direction_u = combine(residual_u, plus_factor, combine(u0, less_omega, u1))
    moved = [[plus_alpha[k] * u0[z][k] + plus_omega[k] * middle_u[z][k]
              for k in range(COMPS)] for z in range(planes)]
    image_image = finish(3, inner_part(image_u))
    start_sums(1, add_products(total, 4, [
        (image_image, residual), (image_image, image),
        (residual_image, image_image), (image_image, image_image)]))
    along, rr, ri, tt, ir, ii, ti, vv = finish_sums(1, 8)
    alpha = rho / along
    omega = ((rr - alpha * ri) - alpha * (ir - alpha * ii)) / (tt - alpha * (2.0 * ti - alpha * vv))
    plus_alpha, plus_omega = scale(alpha), scale(omega)
    less_alpha, less_omega = scale(-alpha), scale(-omega)
    moved = combine(moved, plus_alpha, direction_u)
    moved = combine(moved, plus_omega, combine(residual_u, less_alpha, image_u))
    left = combine(combine(residual, less_alpha, image), less_omega,
                   combine(residual_image, less_alpha, image_image))
    for z in range(planes):
        for k in range(COMPS):
            out_velocity[k, z] = moved[z][k]
            out_residual[k, z] = left[z][k]

    await_bytes(arrived.at[pl.ds(0, count - 1)], part_sems.at[0])
    for which in range(2):
        await_bytes(sums_in.at[which, pl.ds(0, count - 1)], sum_sems.at[which, 0])
    for step in range(STEPS):
        for copy, sends, _ in halo_copies(step):
            pl.when(sends)(copy.wait_send)


def solution(mesh):
    slabs, groups = mesh.shape["slab"], mesh.shape["batch"]
    count = slabs * groups

    def local(velocity_old, courant, cell_ids, forces, weights):
        planes, rows, width = velocity_old.shape[1:]
        per_slab = cell_ids.shape[0] // slabs
        whole = pl.BlockSpec(memory_space=pltpu.VMEM)
        out = jax.ShapeDtypeStruct(velocity_old.shape, jnp.float32)
        f32 = lambda *shape: pltpu.VMEM(shape, jnp.float32)
        edge = (COMPS, rows, width)
        lines = (planes * COMPS, width)
        return pl.pallas_call(
            functools.partial(kernel, slabs, groups),
            out_shape=(out, out),
            in_specs=[whole] * 5,
            out_specs=(whole, whole),
            scratch_shapes=[
                f32(slabs, FIELDS, per_slab), f32(count, FIELDS, per_slab),
                f32(STEPS, 2, *edge), f32(STEPS, *edge), f32(STEPS, *edge),
                f32(STEPS, 2, *lines), f32(STEPS, *lines), f32(STEPS, *lines),
                f32(2, 1, width), f32(2, count, 1, width),
                pltpu.SemaphoreType.DMA((2,)),
                pltpu.SemaphoreType.DMA((STEPS, 4)),
                pltpu.SemaphoreType.DMA((STEPS, 4)),
                pltpu.SemaphoreType.DMA((2, 2)),
            ],
            compiler_params=pltpu.CompilerParams(collective_id=0, has_side_effects=True),
        )(velocity_old, courant, cell_ids.reshape(slabs, per_slab), forces,
          weights.reshape(slabs, per_slab))

    field = P(None, "slab", "batch", None)
    return jax.shard_map(
        local,
        mesh=mesh,
        in_specs=(field, field, P(("slab", "batch")), P(None, ("slab", "batch")), P(("slab", "batch"))),
        out_specs=(field, field),
        check_vma=False,
    )
```

time: 287 us -> 35 us (0.12)
  blocking collectives: 171 us -> 0 us
  waiting for transfers between devices: 48.5 us -> 0 us
  starting transfers between devices: 45.1 us -> 0 us
  Pallas kernels: 0 us -> 32 us
  between operations: 14.5 us -> 0.65 us
  other arithmetic: 3.66 us -> 0 us
    psum x4 -> x0, blocking collectives: 171 us -> none  [the longest x2 85.6 us: local(): closing_sums = lax.psum(jnp.stack(term_list, axis=0), ('slab', 'batch'))]
    ppermute x16 -> x0, starting transfers between devices: 34.4 us -> none  [the longest x8 24.1 us: extended(): lax.ppermute(lax.slice_in_dim(block, block.shape[dim] - width, None, axis...]
    pallas_call x0 -> x1, Pallas kernels: none -> 32 us  [local(): pl.pallas_call(functools.partial(kernel, slabs, groups), out_shape=(out,...]
    ppermute x16 -> x0, waiting for transfers between devices: 20.1 us -> none  [the longest x8 13.9 us: extended(): lax.ppermute(lax.slice_in_dim(block, 0, width, axis=dim), axis, backward)]
    reduce_scatter x1 -> x0, waiting for transfers between devices: 17.2 us -> none  [local(): lax.psum_scatter(deposit_rows(ids_here, moved_momentum, block_rows * lax....]
    all_to_all x2 -> x0, waiting for transfers between devices: 11.3 us -> none  [the longest x1 6.3 us: local(): lax.all_to_all(momentum, 'slab', split_axis=1, concat_axis=1, tiled=True)]
    all_to_all x2 -> x0, starting transfers between devices: 10.7 us -> none  [the longest x1 7.32 us: local(): lax.all_to_all(cell_ids, 'slab', split_axis=0, concat_axis=0, tiled=True)]
  transfers between devices with their start and end apart: 19 -> 0, of which waited for: 11 -> 0; matrix products, arithmetic and copies ran while one was open for 1% -> 0% of each run, Pallas kernels for 0% -> 0%
where the time goes in v1:
time: 35 us; the launch traced here: 34.7 us
  Pallas kernels  32 us (91%)
  local copies, waits for them, and re-layouts  2.06 us (6%)
  between operations  0.65 us (2%)
    pallas_call x1, Pallas kernels, local(): pl.pallas_call(functools.partial(kernel, slabs, groups), out_shape=(out,...  32 us
    unnamed x4, local copies, waits for them, and re-layouts  2.06 us

profile of v1, /device:TPU:0, one launch (start us, length us, event | category | flops | bytes accessed | tf_op | source)
XLA Modules:
  0.0 34.7 jit_solution(17139068345290213837)
XLA Ops:
  0.6 32.0 %shard_map.68 = (f32[3,2,16,128]{3,2,1,0:T(8,128)}, f32[3,2,16,128]{3,2,1,0:T(8,128)}) custom-call(f32[3,2,16,128]{3,2,1,0:T(8,128)} %velocity.1, f32[3,2,16,128]{3,2,1,0:T(8,128)} %courant.1, s32[8,128]{1,0:T(8,128)} %bitcast.2, f32[3,1024]{1,0:T(4,128)} %forces.1, f32[8,128]{1,0:T(8,128)} %bitcast.3), custom_call_target="tpu_custom_call" | custom-call | tf_op jit(solution)/shard_map/pallas_call | solution.py:303
  32.7 0.0 copy-start
  32.7 1.4 %copy.9 = f32[3,2,16,128]{3,2,1,0:T(8,128)} copy(f32[3,2,16,128]{3,2,1,0:T(8,128)} %get-tuple-element.4) | data formatting | bytes 98304
  34.1 0.0 copy-done
  34.1 0.6 %copy.10 = f32[3,2,16,128]{3,2,1,0:T(8,128)} copy(f32[3,2,16,128]{3,2,1,0:T(8,128)S(1)} %copy-done) | data formatting | bytes 98304
Async XLA Ops:
  32.7 1.4 %copy-start = (f32[3,2,16,128]{3,2,1,0:T(8,128)S(1)}, f32[3,2,16,128]{3,2,1,0:T(8,128)}, u32[]{:S(2)}) copy-start(f32[3,2,16,128]{3,2,1,0:T(8,128)} %get-tuple-element.5) | copy-start | bytes 147460

commit v2 on v1

--- a/solution.py
+++ b/solution.py
@@ -18,11 +18,12 @@
 
 def kernel(
     slabs, groups,
+    velocity_in, courant_in, cells_in, forces_in, weights_in,
+    out_velocity, out_residual,
     velocity, courant, cells, forces, weights,
-    out_velocity, out_residual,
     pack, arrived, plane_out, plane_low, plane_high, row_out, row_low, row_high,
     sums_out, sums_in,
-    part_sems, halo_send, halo_recv, sum_sems,
+    load_sems, part_sems, halo_send, halo_recv, sum_sems,
 ):
     planes, rows, width = velocity.shape[1:]
     count = slabs * groups
@@ -39,10 +40,21 @@
             return carry
         lax.fori_loop(1, count, step, 0)
 
+    loads = [
+        pltpu.make_async_copy(source_ref, target_ref, load_sems.at[i])
+        for i, (source_ref, target_ref) in enumerate((
+            (cells_in, cells), (weights_in, weights), (forces_in, forces),
+            (velocity_in, velocity), (courant_in, courant)))
+    ]
+    for load in loads:
+        load.start()
+
     barrier = pltpu.get_barrier_semaphore()
     others(lambda peer: pl.semaphore_signal(
         barrier, inc=1, device_id=place(peer), device_id_type=MESH))
 
+    for load in loads[:3]:
+        load.wait()
     for target in range(slabs):
         span = slice(target * per_slab, (target + 1) * per_slab)
         moved = (weights[target:target + 1, :] * forces[:, span]).astype(jnp.bfloat16)
@@ -68,6 +80,9 @@
         ).start()
 
     others(send_particles)
+
+    for load in loads[3:]:
+        load.wait()
 
     lane = lax.broadcasted_iota(jnp.int32, (rows, width), 1)
     line = lax.broadcasted_iota(jnp.int32, (rows, width), 0)
@@ -241,6 +256,9 @@
     start_halo(2, u2)
     start_sums(0, add_products(total, 3, [(w0, w2), (w1, w2), (w2, w2)]))
     w3 = finish(2, inner_part(u2))
+    u3 = precondition(w3)
+    start_halo(3, u3)
+    w4 = finish(3, inner_part(u3))
     g00, g01, g11, g02, g12, g22 = finish_sums(0, 6)
     alpha = g00 / g01
     omega = ((g01 - alpha * g02) - alpha * (g11 - alpha * g12)) / (g11 - alpha * (2.0 * g12 - alpha * g22))
@@ -251,21 +269,23 @@
     middle_u = combine(u0, less_alpha, u1)
     turned = combine(w1, less_alpha, w2)
     residual = combine(combine(w0, less_alpha, w1), less_omega, turned)
-    residual_u = combine(middle_u, less_omega, combine(u1, less_alpha, u2))
-    residual_image = combine(turned, less_omega, combine(w2, less_alpha, w3))
+    middle_u_image = combine(u1, less_alpha, u2)
+    residual_u = combine(middle_u, less_omega, middle_u_image)
+    middle_image = combine(w2, less_alpha, w3)
+    residual_image = combine(turned, less_omega, middle_image)
+    residual_image2 = combine(middle_image, less_omega, combine(w3, less_alpha, w4))
 
     image = combine(residual_image, plus_factor, combine(w1, less_omega, w2))
-    image_u = precondition(image)
-    start_halo(3, image_u)
-    total = add_products(jnp.zeros((8, width), jnp.float32), 0, [
-        (w0, image), (residual_image, residual), (residual_image, image), (residual_image, residual_image)])
+    image_u = combine(combine(middle_u_image, less_omega, combine(u2, less_alpha, u3)),
+                      plus_factor, combine(u1, less_omega, u2))
+    image_image = combine(residual_image2, plus_factor, combine(w2, less_omega, w3))
+    start_sums(1, add_products(jnp.zeros((8, width), jnp.float32), 0, [
+        (w0, image), (residual_image, residual), (residual_image, image), (residual_image, residual_image),
+        (image_image, residual), (image_image, image),
+        (residual_image, image_image), (image_image, image_image)]))
     direction_u = combine(residual_u, plus_factor, combine(u0, less_omega, u1))
     moved = [[plus_alpha[k] * u0[z][k] + plus_omega[k] * middle_u[z][k]
               for k in range(COMPS)] for z in range(planes)]
-    image_image = finish(3, inner_part(image_u))
-    start_sums(1, add_products(total, 4, [
-        (image_image, residual), (image_image, image),
-        (residual_image, image_image), (image_image, image_image)]))
     along, rr, ri, tt, ir, ii, ti, vv = finish_sums(1, 8)
     alpha = rho / along
     omega = ((rr - alpha * ri) - alpha * (ir - alpha * ii)) / (tt - alpha * (2.0 * ti - alpha * vv))
@@ -288,6 +308,15 @@
             pl.when(sends)(copy.wait_send)
 
 
+def writer(velocity, residual, out_velocity, out_residual, sems):
+    copies = [pltpu.make_async_copy(velocity, out_velocity, sems.at[0]),
+              pltpu.make_async_copy(residual, out_residual, sems.at[1])]
+    for copy in copies:
+        copy.start()
+    for copy in copies:
+        copy.wait()
+
+
 def solution(mesh):
     slabs, groups = mesh.shape["slab"], mesh.shape["batch"]
     count = slabs * groups
@@ -297,19 +326,24 @@
         per_slab = cell_ids.shape[0] // slabs
         whole = pl.BlockSpec(memory_space=pltpu.VMEM)
         out = jax.ShapeDtypeStruct(velocity_old.shape, jnp.float32)
+        held = pltpu.VMEM(velocity_old.shape, jnp.float32)
+        far = pl.BlockSpec(memory_space=pltpu.HBM)
         f32 = lambda *shape: pltpu.VMEM(shape, jnp.float32)
         edge = (COMPS, rows, width)
         lines = (planes * COMPS, width)
-        return pl.pallas_call(
+        results = pl.pallas_call(
             functools.partial(kernel, slabs, groups),
-            out_shape=(out, out),
-            in_specs=[whole] * 5,
+            out_shape=(held, held),
+            in_specs=[far] * 5,
             out_specs=(whole, whole),
             scratch_shapes=[
+                held, held,
+                pltpu.VMEM((slabs, per_slab), jnp.int32), f32(*forces.shape), f32(slabs, per_slab),
                 f32(slabs, FIELDS, per_slab), f32(count, FIELDS, per_slab),
                 f32(STEPS, 2, *edge), f32(STEPS, *edge), f32(STEPS, *edge),
                 f32(STEPS, 2, *lines), f32(STEPS, *lines), f32(STEPS, *lines),
                 f32(2, 1, width), f32(2, count, 1, width),
+                pltpu.SemaphoreType.DMA((5,)),
                 pltpu.SemaphoreType.DMA((2,)),
                 pltpu.SemaphoreType.DMA((STEPS, 4)),
                 pltpu.SemaphoreType.DMA((STEPS, 4)),
@@ -318,6 +352,13 @@
             compiler_params=pltpu.CompilerParams(collective_id=0, has_side_effects=True),
         )(velocity_old, courant, cell_ids.reshape(slabs, per_slab), forces,
           weights.reshape(slabs, per_slab))
+        return pl.pallas_call(
+            writer,
+            out_shape=(out, out),
+            in_specs=[whole] * 2,
+            out_specs=(far, far),
+            scratch_shapes=[pltpu.SemaphoreType.DMA((2,))],
+        )(*[pltpu.with_memory_space_constraint(r, pltpu.VMEM) for r in results])
 
     field = P(None, "slab", "batch", None)
     return jax.shard_map(

time: 35 us -> 31.8 us (0.909)
  local copies, waits for them, and re-layouts: 2.06 us -> 0 us
  Pallas kernels: 32 us -> 30.9 us
    unnamed x4 -> x0, local copies, waits for them, and re-layouts: 2.06 us -> none
    pallas_call x1 -> x2, Pallas kernels: 32 us -> 30.9 us  [the longest x1 30.3 us: local(): pl.pallas_call(functools.partial(kernel, slabs, groups), out_shape=(held,...]
where the time goes in v2:
time: 31.8 us; the launch traced here: 31.6 us
  Pallas kernels  30.9 us (97%)
  between operations  0.64 us (2%)
    pallas_call x1, Pallas kernels, local(): pl.pallas_call(functools.partial(kernel, slabs, groups), out_shape=(held,...  30.3 us
    pallas_call x1, Pallas kernels, local(): pl.pallas_call(writer, out_shape=(out, out), in_specs=[whole] * 2, out_sp...  0.66 us

profile of v2, /device:TPU:0, one launch (start us, length us, event | category | flops | bytes accessed | tf_op | source)
XLA Modules:
  0.0 31.6 jit_solution(10608838357207357694)
XLA Ops:
  0.6 30.3 %shard_map.68 = (f32[3,2,16,128]{3,2,1,0:T(8,128)S(1)}, f32[3,2,16,128]{3,2,1,0:T(8,128)S(1)}) custom-call(f32[3,2,16,128]{3,2,1,0:T(8,128)} %velocity_in.1, f32[3,2,16,128]{3,2,1,0:T(8,128)} %courant_in.1, s32[8,128]{1,0:T(8,128)} %bitcast.2, f32[3,1024]{1,0:T(4,128)} %forces_in.1, f32[8,128]{1,0:T(8,128)} %bitcast.3), custom_call_target="tpu_custom_call" | custom-call | tf_op jit(solution)/shard_map/pallas_call | solution.py:334
  30.9 0.7 %shard_map.69 = (f32[3,2,16,128]{3,2,1,0:T(8,128)}, f32[3,2,16,128]{3,2,1,0:T(8,128)}) custom-call(f32[3,2,16,128]{3,2,1,0:T(8,128)S(1)} %get-tuple-element.4.velocity, f32[3,2,16,128]{3,2,1,0:T(8,128)S(1)} %get-tuple-element.5.residual), custom_call_target="tpu_custom_call" | custom-call | tf_op jit(solution)/shard_map/pallas_call | solution.py:355

commit v3 on v2

--- a/solution.py
+++ b/solution.py
@@ -46,12 +46,11 @@
             (cells_in, cells), (weights_in, weights), (forces_in, forces),
             (velocity_in, velocity), (courant_in, courant)))
     ]
-    for load in loads:
-        load.start()
-
     barrier = pltpu.get_barrier_semaphore()
     others(lambda peer: pl.semaphore_signal(
         barrier, inc=1, device_id=place(peer), device_id_type=MESH))
+    for load in loads:
+        load.start()
 
     for load in loads[:3]:
         load.wait()

time: 31.8 us -> 31.7 us (level)
  no operation moved by 1% of the time
where the time goes in v3:
time: 31.7 us; the launch traced here: 31.6 us
  Pallas kernels  30.9 us (97%)
  between operations  0.64 us (2%)
    pallas_call x1, Pallas kernels, local(): pl.pallas_call(functools.partial(kernel, slabs, groups), out_shape=(held,...  30.3 us
    pallas_call x1, Pallas kernels, local(): pl.pallas_call(writer, out_shape=(out, out), in_specs=[whole] * 2, out_sp...  0.66 us

profile of v3, /device:TPU:0, one launch (start us, length us, event | category | flops | bytes accessed | tf_op | source)
XLA Modules:
  0.0 31.6 jit_solution(1688648474100978864)
XLA Ops:
  0.6 30.3 %shard_map.68 = (f32[3,2,16,128]{3,2,1,0:T(8,128)S(1)}, f32[3,2,16,128]{3,2,1,0:T(8,128)S(1)}) custom-call(f32[3,2,16,128]{3,2,1,0:T(8,128)} %velocity_in.1, f32[3,2,16,128]{3,2,1,0:T(8,128)} %courant_in.1, s32[8,128]{1,0:T(8,128)} %bitcast.2, f32[3,1024]{1,0:T(4,128)} %forces_in.1, f32[8,128]{1,0:T(8,128)} %bitcast.3), custom_call_target="tpu_custom_call" | custom-call | tf_op jit(solution)/shard_map/pallas_call | solution.py:333
  30.9 0.7 %shard_map.69 = (f32[3,2,16,128]{3,2,1,0:T(8,128)}, f32[3,2,16,128]{3,2,1,0:T(8,128)}) custom-call(f32[3,2,16,128]{3,2,1,0:T(8,128)S(1)} %get-tuple-element.4.velocity, f32[3,2,16,128]{3,2,1,0:T(8,128)S(1)} %get-tuple-element.5.residual), custom_call_target="tpu_custom_call" | custom-call | tf_op jit(solution)/shard_map/pallas_call | solution.py:354
